TPU v7x, 32 devices: a whole 2x2x4 slice. The times are simulated.
32 devices in a mesh: pos: 8 (over z, y), head: 4 (over x, core).
Axes of the slice: x: 2, y: 2, z: 4, core: 2. Of those that a mesh axis runs over, the one named last changes fastest.
Arguments:
- queries: bfloat16 [32, 512, 768], P('head', 'pos'), may hold values from -102 to 102
- latents: bfloat16 [32, 256, 1280], P('head', 'pos'), may hold values from -6 to 6
- w_query: bfloat16 [768, 768], replicated, may hold values from -0.21875 to 0.21875
- kv_gain: float32 [1280], replicated, may hold values from 0.1 to 1.9
- w_kv: bfloat16 [1280, 1536], replicated, may hold values from -0.15625 to 0.15625
- w_out: bfloat16 [768, 768], replicated, may hold values from -0.21875 to 0.21875
- mlp_gain: float32 [768], replicated, may hold values from 0.1 to 1.9
- w_up: bfloat16 [768, 768], replicated, may hold values from -0.21875 to 0.21875
- w_down: bfloat16 [768, 768], replicated, may hold values from -0.21875 to 0.21875
- w_vocab: bfloat16 [768, 262], replicated, may hold values from -0.59765625 to 0.59765625
- vocab_bias: float32 [262], replicated, may hold values from -4 to 4
- targets: int32 [32, 512], P('head', 'pos'), may hold values from 0 to 261
- mask: int32 [32, 512], P('head', 'pos'), may hold values from 0 to 1, as said below
Outputs:
- logits: bfloat16 [32, 512, 262], P('head', 'pos')
- loss: float32 [], replicated
Inputs may be any that keep to these rules, and one draw needn't show every extreme that they name: `mask`: every sequence has at least one masked position.
All inputs are finite; a program needn't handle non-finite values.
Results may differ from a plain program's by a relative error of at most 0.0085.
Values may be sent and summed in bfloat16 or wider, within the bound.
A program may use at most 64 MiB of HBM per device.

v0:
```python
import functools

import jax
import jax.numpy as jnp
from jax import lax
from jax.experimental import pallas as pl
from jax.experimental.pallas import tpu as pltpu
from jax.sharding import PartitionSpec as P

HEADS = 8
LAT_SPLIT = 1
ROW_SPLIT = 1
epsilon = 1e-05
MESH = pl.DeviceIdType.MESH


def layer_norm(field, gain):
    centre = field - jnp.mean(field, axis=-1, keepdims=True)
    spread = jnp.mean(centre * centre, axis=-1, keepdims=True)
    return centre * lax.rsqrt(spread + epsilon) * gain


def dot(left, right):
    return jnp.dot(left, right, preferred_element_type=jnp.float32)


def dot_last(left, right):
    return lax.dot_general(
        left, right, (((1,), (1,)), ((), ())), preferred_element_type=jnp.float32
    )


def kernel(
    n_pos,
    n_head,
    group,
    seqs,
    queries,
    latents,
    w_query_hbm,
    kv_gain,
    w_kv_hbm,
    w_out_hbm,
    mlp_gain,
    w_up_hbm,
    w_down_hbm,
    w_vocab_hbm,
    vocab_bias,
    targets,
    mask,
    out,
    loss_out,
    lat_stage,
    q_stage,
    lat_buf,
    q_buf,
    t_buf,
    m_buf,
    w_query,
    w_kv,
    w_out,
    w_up,
    w_down,
    w_vocab,
    kv_buf,
    logit_buf,
    acc,
    part_src,
    part_all,
    total_src,
    total_all,
    lat_send,
    lat_recv,
    q_send,
    q_recv,
    t_send,
    t_recv,
    m_send,
    m_recv,
    out_send,
    out_recv,
    p_send,
    p_recv,
    h_send,
    h_recv,
    w_sem,
    stage_sem,
):
    me = lax.axis_index("pos")
    my_head = lax.axis_index("head")
    mine = lax.rem(me, group)
    base = me - mine

    def pos_peer(k):
        return lax.rem(base + (k // group) * group, n_pos) + lax.rem(mine + k % group, group)

    def group_peer(k):
        return base + lax.rem(mine + k, group)

    def group_source(k):
        return base + lax.rem(mine + group - k, group)

    barrier = pltpu.get_barrier_semaphore()
    for k in range(1, n_pos):
        pl.semaphore_signal(barrier, inc=1, device_id={"pos": pos_peer(k)}, device_id_type=MESH)
    for k in range(1, n_head):
        pl.semaphore_signal(
            barrier, inc=1, device_id={"head": lax.rem(my_head + k, n_head)}, device_id_type=MESH
        )

    staged = (
        pltpu.make_async_copy(latents, lat_stage, stage_sem.at[0]),
        pltpu.make_async_copy(queries, q_stage, stage_sem.at[1]),
    )
    for copy in staged:
        copy.start()
    local = []

    def start_local(src, dst, sem):
        copy = pltpu.make_async_copy(src, dst, sem)
        copy.start()
        local.append(copy)

    start_local(queries.at[pl.ds(mine * seqs, seqs)], q_buf.at[0], q_recv.at[0])
    start_local(targets, t_buf.at[0], t_recv.at[0])
    start_local(mask, m_buf.at[0], m_recv.at[0])
    pairs = (
        (w_query_hbm, w_query),
        (w_kv_hbm, w_kv),
        (w_out_hbm, w_out),
        (w_up_hbm, w_up),
        (w_down_hbm, w_down),
        (w_vocab_hbm, w_vocab),
    )
    for index, (src, dst) in enumerate(pairs):
        start_local(src, dst, w_sem.at[index])

    def lat_copy(k, i):
        peer = pos_peer(k)
        return pltpu.make_async_remote_copy(
            src_ref=lat_stage.at[lax.rem(peer, group) * seqs + i],
            dst_ref=lat_buf.at[i, k],
            send_sem=lat_send.at[i, k],
            recv_sem=lat_recv.at[i, k],
            device_id={"pos": peer},
            device_id_type=MESH,
        )

    def lat_local(i):
        return pltpu.make_async_copy(
            latents.at[mine * seqs + i], lat_buf.at[i, 0], lat_recv.at[i, 0]
        )

    def group_copy(k, src, dst, send, recv):
        return pltpu.make_async_remote_copy(
            src_ref=src,
            dst_ref=dst,
            send_sem=send.at[k],
            recv_sem=recv.at[k],
            device_id={"pos": group_peer(k)},
            device_id_type=MESH,
        )

    def q_copy(k):
        peer = lax.rem(mine + k, group)
        return group_copy(k, q_stage.at[pl.ds(peer * seqs, seqs)], q_buf.at[k], q_send, q_recv)

    def t_copy(k):
        return group_copy(k, targets, t_buf.at[k], t_send, t_recv)

    def m_copy(k):
        return group_copy(k, mask, m_buf.at[k], m_send, m_recv)

    def out_copy(k, i):
        return pltpu.make_async_remote_copy(
            src_ref=logit_buf.at[i, k],
            dst_ref=out.at[mine * seqs + i],
            send_sem=out_send.at[i, k],
            recv_sem=out_recv.at[i, k],
            device_id={"pos": group_source(k)},
            device_id_type=MESH,
        )

    def out_local(i):
        return pltpu.make_async_copy(
            logit_buf.at[i, 0], out.at[mine * seqs + i], out_recv.at[i, 0]
        )

    for i in range(seqs):
        lat_local(i).start()

    for copy in staged:
        copy.wait()
    pl.semaphore_wait(barrier, n_pos - 1 + n_head - 1)

    for k in range(1, n_pos):
        lat_copy(k, 0).start()
    for k in range(1, group):
        q_copy(k).start()
        t_copy(k).start()
        m_copy(k).start()
    for k in range(1, n_pos):
        lat_copy(k, 1).start()

    for copy in local:
        copy.wait()
    for k in range(1, group):
        q_copy(k).wait_recv()
        t_copy(k).wait_recv()
        m_copy(k).wait_recv()

    rows_dev = q_buf.shape[2]
    width = q_buf.shape[3]
    rows_all = group * rows_dev
    lat_dev = lat_buf.shape[2]
    lat_split, row_split = LAT_SPLIT, ROW_SPLIT
    lat_width = lat_buf.shape[3]
    head_dim = width // HEADS
    scale_factor = float(head_dim) ** (-0.5)
    vocab = w_vocab.shape[0]
    lanes = 128
    acc[...] = jnp.zeros_like(acc)

    columns = []
    for k in range(group):
        code = (t_buf[k] + vocab * m_buf[k]).astype(jnp.float32)
        pad = -rows_dev % lanes
        if pad:
            code = jnp.concatenate(
                [code, jnp.zeros((code.shape[0], pad), jnp.float32)], axis=1
            )
        columns.append(code.T[:rows_dev])
    code_cols = jnp.concatenate(columns, axis=0)

    def one_sequence(i, carry):
        seq_queries = q_buf[:, i].reshape(rows_all, width)
        query_all = dot(seq_queries, w_query[...]).astype(jnp.bfloat16)

        chunk = 256
        step = n_pos // lat_split
        lat_rows = step * lat_dev
        for part in reversed(range(lat_split)):
            for k in reversed(range(part * step, (part + 1) * step)):
                if k == 0:
                    lat_local(i).wait()
                else:
                    lat_copy(k, i).wait_recv()
            field = lat_buf[i, part * step : (part + 1) * step].astype(jnp.float32)
            field = field.reshape(lat_rows, lat_width)
            normed_lat = layer_norm(field, kv_gain[...].reshape(1, lat_width)).astype(jnp.bfloat16)
            for start in range(0, 2 * width, chunk):
                kv_buf[part * lat_rows : (part + 1) * lat_rows, start : start + chunk] = dot(
                    normed_lat, w_kv[:, start : start + chunk]
                ).astype(jnp.bfloat16)

        for part in reversed(range(row_split)):
            decode(i, part, query_all)
        return carry

    def decode(i, part, query_all):
        members = group // row_split
        begin_slot = part * members
        rows = members * rows_dev
        begin_row = begin_slot * rows_dev
        query_proj = query_all[begin_row : begin_row + rows]
        seq_queries = q_buf[begin_slot : begin_slot + members, i].reshape(rows, width)
        code_all = code_cols[begin_row : begin_row + rows]

        tiles = [None] * (width // lanes)
        for h in range(HEADS):
            low, high = h * head_dim, (h + 1) * head_dim
            first_tile, last_tile = low // lanes, (high - 1) // lanes
            begin, end = first_tile * lanes, (last_tile + 1) * lanes
            lane = lax.broadcasted_iota(jnp.int32, (1, end - begin), 1) + begin
            inside = jnp.logical_and(lane >= low, lane < high).astype(jnp.bfloat16)
            keys = kv_buf[:, begin:end] * inside
            values = kv_buf[:, width + begin : width + end] * inside
            scores = (
                dot_last(query_proj[:, begin:end], keys) * scale_factor
            )
            power = jnp.exp(scores - jnp.max(scores, axis=-1, keepdims=True))
            weights = (power / jnp.sum(power, axis=-1, keepdims=True)).astype(jnp.bfloat16)
            part = dot(weights, values)
            for t in range(first_tile, last_tile + 1):
                piece = part[:, t * lanes - begin : (t + 1) * lanes - begin]
                tiles[t] = piece if tiles[t] is None else tiles[t] + piece
        attended = jnp.concatenate([tile.astype(jnp.bfloat16) for tile in tiles], axis=1)

        first = seq_queries.astype(jnp.float32) + dot(attended, w_out[...])
        normed = layer_norm(first, mlp_gain[...].reshape(1, width)).astype(jnp.bfloat16)
        hidden = jax.nn.gelu(dot(normed, w_up[...])).astype(jnp.bfloat16)
        output = (first + dot(hidden, w_down[...])).astype(jnp.bfloat16)
        full_logits = dot_last(output, w_vocab[...]) + vocab_bias[...].reshape(1, vocab)
        logit_buf[i, begin_slot : begin_slot + members] = full_logits.astype(jnp.bfloat16).reshape(
            members, rows_dev, vocab
        )

        code_lane = lax.broadcasted_iota(jnp.int32, code_all.shape, 1)
        code = jnp.sum(
            jnp.where(code_lane == mine * seqs + i, code_all, 0.0), axis=1, keepdims=True
        )
        weight_mask = (code >= float(vocab)).astype(jnp.float32)
        target = (code - float(vocab) * weight_mask).astype(jnp.int32)
        ids = lax.broadcasted_iota(jnp.int32, full_logits.shape, 1)
        picked = jnp.sum(jnp.where(ids == target, full_logits, 0.0), axis=1, keepdims=True)
        top = jnp.max(full_logits, axis=1, keepdims=True)
        spread = jnp.log(jnp.sum(jnp.exp(full_logits - top), axis=1, keepdims=True))
        cross = top + spread - picked

        for k in range(begin_slot, begin_slot + members):
            @pl.when(i < seqs - 1)
            def send(k=k):
                if k == 0:
                    out_local(i).start()
                else:
                    out_copy(k, i).start()

        loss_sum = jnp.sum(cross * weight_mask, axis=0, keepdims=True)
        mask_sum = jnp.sum(weight_mask, axis=0, keepdims=True)
        place = lax.broadcasted_iota(jnp.int32, acc.shape, 1)
        acc[...] += jnp.where(place == 0, loss_sum, jnp.where(place == 1, mask_sum, 0.0))

    lax.fori_loop(0, seqs, one_sequence, 0)

    def p_copy(k):
        return pltpu.make_async_remote_copy(
            src_ref=part_src,
            dst_ref=part_all.at[me],
            send_sem=p_send.at[k],
            recv_sem=p_recv.at[k],
            device_id={"pos": pos_peer(k)},
            device_id_type=MESH,
        )

    def h_copy(k):
        return pltpu.make_async_remote_copy(
            src_ref=total_src,
            dst_ref=total_all.at[my_head],
            send_sem=h_send.at[k],
            recv_sem=h_recv.at[k],
            device_id={"head": lax.rem(my_head + k, n_head)},
            device_id_type=MESH,
        )

    part = acc[...]
    part_src[...] = part
    part_all[me] = part
    for k in range(n_pos - 1, 0, -1):
        p_copy(k).start()
    for k in range(1, group):
        out_copy(k, seqs - 1).start()
    out_local(seqs - 1).start()
    for k in range(1, n_pos):
        p_copy(k).wait_recv()
    total = part_all[0]
    for index in range(1, n_pos):
        total = total + part_all[index]
    total_src[...] = total
    total_all[my_head] = total
    for k in range(1, n_head):
        h_copy(k).start()
    for k in range(1, n_head):
        h_copy(k).wait_recv()
    whole = total_all[0]
    for index in range(1, n_head):
        whole = whole + total_all[index]
    loss_out[...] = whole[:, 0:1] / whole[:, 1:2]

    for k in range(1, n_pos):
        p_copy(k).wait_send()
    for k in range(1, n_head):
        h_copy(k).wait_send()
    for k in range(1, group):
        q_copy(k).wait_send()
        t_copy(k).wait_send()
        m_copy(k).wait_send()
    for i in range(seqs):
        for k in range(1, n_pos):
            lat_copy(k, i).wait_send()
        out_local(i).wait()
        for k in range(1, group):
            out_copy(k, i).wait()


def on_device(n_pos, n_head, *args):
    (queries, latents, w_query, kv_gain, w_kv, w_out, mlp_gain, w_up, w_down, w_vocab, vocab_bias, targets, mask) = args
    batch_dev, pos_dev, width = queries.shape
    lat_dev, lat_width = latents.shape[1:]
    vocab = w_vocab.shape[1]
    group = max(1, min(n_pos, batch_dev) // 2)
    seqs = batch_dev // group
    assert n_pos % group == 0 and batch_dev % group == 0
    hbm = pl.BlockSpec(memory_space=pltpu.HBM)
    vmem = pl.BlockSpec(memory_space=pltpu.VMEM)
    dma = pltpu.SemaphoreType.DMA
    bf16, f32 = jnp.bfloat16, jnp.float32
    logits, loss = pl.pallas_call(
        functools.partial(kernel, n_pos, n_head, group, seqs),
        out_shape=(
            jax.ShapeDtypeStruct((batch_dev, pos_dev, vocab), bf16),
            jax.ShapeDtypeStruct((1, 1), f32),
        ),
        in_specs=[hbm, hbm, hbm, vmem, hbm, hbm, vmem, hbm, hbm, hbm, vmem, hbm, hbm],
        out_specs=(pl.BlockSpec(memory_space=pl.ANY), vmem),
        scratch_shapes=[
            pltpu.VMEM(latents.shape, bf16),
            pltpu.VMEM(queries.shape, bf16),
            pltpu.VMEM((seqs, n_pos, lat_dev, lat_width), bf16),
            pltpu.VMEM((group, seqs, pos_dev, width), bf16),
            pltpu.VMEM((group, batch_dev, pos_dev), jnp.int32),
            pltpu.VMEM((group, batch_dev, pos_dev), jnp.int32),
            pltpu.VMEM(w_query.shape, bf16),
            pltpu.VMEM(w_kv.shape, bf16),
            pltpu.VMEM(w_out.shape, bf16),
            pltpu.VMEM(w_up.shape, bf16),
            pltpu.VMEM(w_down.shape, bf16),
            pltpu.VMEM(w_vocab.shape[::-1], bf16),
            pltpu.VMEM((n_pos * lat_dev, 2 * width), bf16),
            pltpu.VMEM((seqs, group, pos_dev, vocab), bf16),
            pltpu.VMEM((1, 128), f32),
            pltpu.VMEM((1, 128), f32),
            pltpu.VMEM((n_pos, 1, 128), f32),
            pltpu.VMEM((1, 128), f32),
            pltpu.VMEM((n_head, 1, 128), f32),
            dma((seqs, n_pos)),
            dma((seqs, n_pos)),
            dma((group,)),
            dma((group,)),
            dma((group,)),
            dma((group,)),
            dma((group,)),
            dma((group,)),
            dma((seqs, group)),
            dma((seqs, group)),
            dma((n_pos,)),
            dma((n_pos,)),
            dma((n_head,)),
            dma((n_head,)),
            dma((6,)),
            dma((2,)),
        ],
        compiler_params=pltpu.CompilerParams(
            collective_id=0, has_side_effects=True, vmem_limit_bytes=60 * 1024 * 1024
        ),
    )(
        queries,
        latents,
        w_query,
        kv_gain,
        w_kv,
        w_out,
        mlp_gain,
        w_up,
        w_down,
        w_vocab.T,
        vocab_bias,
        targets,
        mask,
    )
    return (logits, loss.reshape(()))


def solution(mesh):
    in_specs = (
        P("head", "pos", None),
        P("head", "pos", None),
        P(),
        P(),
        P(),
        P(),
        P(),
        P(),
        P(),
        P(),
        P(),
        P("head", "pos"),
        P("head", "pos"),
    )
    out_specs = (P("head", "pos", None), P())
    return jax.shard_map(
        functools.partial(on_device, mesh.shape["pos"], mesh.shape["head"]),
        mesh=mesh,
        in_specs=in_specs,
        out_specs=out_specs,
        check_vma=False,
    )
```

profile of v0, /device:TPU:0, one launch (start us, length us, event | category | flops | bytes accessed | tf_op | source)
XLA Modules:
  0.0 58.4 jit_solution(16124045818195016950)
XLA Ops:
  0.6 54.2 %shard_map.140 = (bf16[8,64,262]{2,1,0:T(8,128)(2,1)}, f32[1,1]{1,0:T(1,128)}) custom-call(bf16[8,64,768]{2,1,0:T(8,128)(2,1)} %queries.1, bf16[8,32,1280]{2,1,0:T(8,128)(2,1)} %latents.1, bf16[768,768]{1,0:T(8,128)(2,1)} %w_query_hbm.1, f32[1280]{0:T(1024)} %kv_gain.1, bf16[1280,1536]{1,0:T(8,128)(2,1)} %w_kv_hbm.1, bf16[768,768]{1,0:T(8,128)(2,1)} %w_out_hbm.1, ...), custom_call_target="tpu_custom_call" | custom-call | tf_op jit(solution)/shard_map/pallas_call | solution.py:397
  54.8 1.8 %copy.17 = bf16[8,64,262]{2,1,0:T(8,128)(2,1)} copy(bf16[8,64,262]{2,1,0:T(8,128)(2,1)} %get-tuple-element.8) | data formatting | bytes 536576
where the time goes:
time: 58.6 us; the launch traced here: 58.4 us
  Pallas kernels  54.2 us (92%)
  between operations  2.4 us (4%)
  local copies, waits for them, and re-layouts  1.78 us (3%)
    pallas_call x1, Pallas kernels, on_device(): pl.pallas_call(functools.partial(kernel, n_pos, n_head, group, seqs), out...  54.2 us
    unnamed x1, local copies, waits for them, and re-layouts  1.78 us

commit v1 on v0

--- a/solution.py
+++ b/solution.py
@@ -67,8 +67,6 @@
     acc,
     part_src,
     part_all,
-    total_src,
-    total_all,
     lat_send,
     lat_recv,
     q_send,
@@ -81,10 +79,9 @@
     out_recv,
     p_send,
     p_recv,
-    h_send,
-    h_recv,
     w_sem,
     stage_sem,
+    stage_sems,
 ):
     me = lax.axis_index("pos")
     my_head = lax.axis_index("head")
@@ -100,13 +97,51 @@
     def group_source(k):
         return base + lax.rem(mine + group - k, group)
 
+    block = max(1, group // 2)
+    n_rows = n_pos // block
+    staged_entry = 2 < n_rows <= 4
+    row = me // block
+    spot = lax.rem(me, block)
+
+    def near(peer):
+        gap = peer // block - row
+        return jnp.logical_and(gap >= -1, gap <= 1)
+
+    def signal_near(semaphore):
+        for k in range(1, block):
+            pl.semaphore_signal(
+                semaphore,
+                inc=1,
+                device_id={"pos": row * block + lax.rem(spot + k, block)},
+                device_id_type=MESH,
+            )
+        for shift, inside in ((-1, row > 0), (1, row < n_rows - 1)):
+
+            @pl.when(inside)
+            def neighbours(shift=shift):
+                for k in range(block):
+                    pl.semaphore_signal(
+                        semaphore,
+                        inc=1,
+                        device_id={"pos": (row + shift) * block + k},
+                        device_id_type=MESH,
+                    )
+
     barrier = pltpu.get_barrier_semaphore()
-    for k in range(1, n_pos):
-        pl.semaphore_signal(barrier, inc=1, device_id={"pos": pos_peer(k)}, device_id_type=MESH)
     for k in range(1, n_head):
         pl.semaphore_signal(
             barrier, inc=1, device_id={"head": lax.rem(my_head + k, n_head)}, device_id_type=MESH
         )
+    if staged_entry:
+        signal_near(barrier)
+        ends = (row > 0).astype(jnp.int32) + (row < n_rows - 1).astype(jnp.int32)
+        n_near = block - 1 + block * ends
+    else:
+        for k in range(1, n_pos):
+            pl.semaphore_signal(
+                barrier, inc=1, device_id={"pos": pos_peer(k)}, device_id_type=MESH
+            )
+        n_near = n_pos - 1
 
     staged = (
         pltpu.make_async_copy(latents, lat_stage, stage_sem.at[0]),
@@ -124,6 +159,84 @@
     start_local(queries.at[pl.ds(mine * seqs, seqs)], q_buf.at[0], q_recv.at[0])
     start_local(targets, t_buf.at[0], t_recv.at[0])
     start_local(mask, m_buf.at[0], m_recv.at[0])
+    def lat_copy(k, i):
+        peer = pos_peer(k)
+        return pltpu.make_async_remote_copy(
+            src_ref=lat_stage.at[lax.rem(peer, group) * seqs + i],
+            dst_ref=lat_buf.at[i, k],
+            send_sem=lat_send.at[i, k],
+            recv_sem=lat_recv.at[i, k],
+            device_id={"pos": peer},
+            device_id_type=MESH,
+        )
+
+    def lat_local(i):
+        return pltpu.make_async_copy(
+            latents.at[mine * seqs + i], lat_buf.at[i, 0], lat_recv.at[i, 0]
+        )
+
+    def group_copy(k, src, dst, send, recv):
+        return pltpu.make_async_remote_copy(
+            src_ref=src,
+            dst_ref=dst,
+            send_sem=send.at[k],
+            recv_sem=recv.at[k],
+            device_id={"pos": group_peer(k)},
+            device_id_type=MESH,
+        )
+
+    def q_copy(k):
+        peer = lax.rem(mine + k, group)
+        return group_copy(k, q_stage.at[pl.ds(peer * seqs, seqs)], q_buf.at[k], q_send, q_recv)
+
+    def t_copy(k):
+        return group_copy(k, targets, t_buf.at[k], t_send, t_recv)
+
+    def m_copy(k):
+        return group_copy(k, mask, m_buf.at[k], m_send, m_recv)
+
+    def out_copy(k, i):
+        return pltpu.make_async_remote_copy(
+            src_ref=logit_buf.at[i, k],
+            dst_ref=out.at[mine * seqs + i],
+            send_sem=out_send.at[i, k],
+            recv_sem=out_recv.at[i, k],
+            device_id={"pos": group_source(k)},
+            device_id_type=MESH,
+        )
+
+    def out_local(i):
+        return pltpu.make_async_copy(
+            logit_buf.at[i, 0], out.at[mine * seqs + i], out_recv.at[i, 0]
+        )
+
+    for i in range(seqs):
+        lat_local(i).start()
+
+    pl.semaphore_wait(barrier, n_near + n_head - 1)
+    for copy in staged:
+        copy.wait()
+
+    cross = tuple(range(group, n_pos))
+    inner = tuple(range(1, group))
+    if staged_entry:
+        for k in cross + inner:
+
+            @pl.when(near(pos_peer(k)))
+            def first(k=k):
+                lat_copy(k, 0).start()
+
+        for stage in range(n_rows - 2):
+            signal_near(stage_sems.at[stage])
+            pl.semaphore_wait(stage_sems.at[stage], n_near)
+        for k in cross + inner:
+
+            @pl.when(jnp.logical_not(near(pos_peer(k))))
+            def second(k=k):
+                lat_copy(k, 0).start()
+    else:
+        for k in cross + inner:
+            lat_copy(k, 0).start()
     pairs = (
         (w_query_hbm, w_query),
         (w_kv_hbm, w_kv),
@@ -135,71 +248,11 @@
     for index, (src, dst) in enumerate(pairs):
         start_local(src, dst, w_sem.at[index])
 
-    def lat_copy(k, i):
-        peer = pos_peer(k)
-        return pltpu.make_async_remote_copy(
-            src_ref=lat_stage.at[lax.rem(peer, group) * seqs + i],
-            dst_ref=lat_buf.at[i, k],
-            send_sem=lat_send.at[i, k],
-            recv_sem=lat_recv.at[i, k],
-            device_id={"pos": peer},
-            device_id_type=MESH,
-        )
-
-    def lat_local(i):
-        return pltpu.make_async_copy(
-            latents.at[mine * seqs + i], lat_buf.at[i, 0], lat_recv.at[i, 0]
-        )
-
-    def group_copy(k, src, dst, send, recv):
-        return pltpu.make_async_remote_copy(
-            src_ref=src,
-            dst_ref=dst,
-            send_sem=send.at[k],
-            recv_sem=recv.at[k],
-            device_id={"pos": group_peer(k)},
-            device_id_type=MESH,
-        )
-
-    def q_copy(k):
-        peer = lax.rem(mine + k, group)
-        return group_copy(k, q_stage.at[pl.ds(peer * seqs, seqs)], q_buf.at[k], q_send, q_recv)
-
-    def t_copy(k):
-        return group_copy(k, targets, t_buf.at[k], t_send, t_recv)
-
-    def m_copy(k):
-        return group_copy(k, mask, m_buf.at[k], m_send, m_recv)
-
-    def out_copy(k, i):
-        return pltpu.make_async_remote_copy(
-            src_ref=logit_buf.at[i, k],
-            dst_ref=out.at[mine * seqs + i],
-            send_sem=out_send.at[i, k],
-            recv_sem=out_recv.at[i, k],
-            device_id={"pos": group_source(k)},
-            device_id_type=MESH,
-        )
-
-    def out_local(i):
-        return pltpu.make_async_copy(
-            logit_buf.at[i, 0], out.at[mine * seqs + i], out_recv.at[i, 0]
-        )
-
-    for i in range(seqs):
-        lat_local(i).start()
-
-    for copy in staged:
-        copy.wait()
-    pl.semaphore_wait(barrier, n_pos - 1 + n_head - 1)
-
-    for k in range(1, n_pos):
-        lat_copy(k, 0).start()
     for k in range(1, group):
         q_copy(k).start()
         t_copy(k).start()
         m_copy(k).start()
-    for k in range(1, n_pos):
+    for k in cross + inner:
         lat_copy(k, 1).start()
 
     for copy in local:
@@ -322,54 +375,35 @@
 
     lax.fori_loop(0, seqs, one_sequence, 0)
 
+    n_all = n_pos * n_head
+    rank = me * n_head + my_head
+
     def p_copy(k):
+        peer = lax.rem(rank + k, n_all)
         return pltpu.make_async_remote_copy(
             src_ref=part_src,
-            dst_ref=part_all.at[me],
+            dst_ref=part_all.at[rank],
             send_sem=p_send.at[k],
             recv_sem=p_recv.at[k],
-            device_id={"pos": pos_peer(k)},
-            device_id_type=MESH,
-        )
-
-    def h_copy(k):
-        return pltpu.make_async_remote_copy(
-            src_ref=total_src,
-            dst_ref=total_all.at[my_head],
-            send_sem=h_send.at[k],
-            recv_sem=h_recv.at[k],
-            device_id={"head": lax.rem(my_head + k, n_head)},
+            device_id={"pos": peer // n_head, "head": lax.rem(peer, n_head)},
             device_id_type=MESH,
         )
 
     part = acc[...]
     part_src[...] = part
-    part_all[me] = part
-    for k in range(n_pos - 1, 0, -1):
+    part_all[rank] = part
+    for k in range(1, n_all):
         p_copy(k).start()
     for k in range(1, group):
         out_copy(k, seqs - 1).start()
     out_local(seqs - 1).start()
-    for k in range(1, n_pos):
+    for k in range(1, n_all):
         p_copy(k).wait_recv()
-    total = part_all[0]
-    for index in range(1, n_pos):
-        total = total + part_all[index]
-    total_src[...] = total
-    total_all[my_head] = total
-    for k in range(1, n_head):
-        h_copy(k).start()
-    for k in range(1, n_head):
-        h_copy(k).wait_recv()
-    whole = total_all[0]
-    for index in range(1, n_head):
-        whole = whole + total_all[index]
+    whole = jnp.sum(part_all[...], axis=0)
     loss_out[...] = whole[:, 0:1] / whole[:, 1:2]
 
-    for k in range(1, n_pos):
+    for k in range(1, n_all):
         p_copy(k).wait_send()
-    for k in range(1, n_head):
-        h_copy(k).wait_send()
     for k in range(1, group):
         q_copy(k).wait_send()
         t_copy(k).wait_send()
@@ -419,9 +453,7 @@
             pltpu.VMEM((seqs, group, pos_dev, vocab), bf16),
             pltpu.VMEM((1, 128), f32),
             pltpu.VMEM((1, 128), f32),
-            pltpu.VMEM((n_pos, 1, 128), f32),
-            pltpu.VMEM((1, 128), f32),
-            pltpu.VMEM((n_head, 1, 128), f32),
+            pltpu.VMEM((n_pos * n_head, 1, 128), f32),
             dma((seqs, n_pos)),
             dma((seqs, n_pos)),
             dma((group,)),
@@ -432,12 +464,11 @@
             dma((group,)),
             dma((seqs, group)),
             dma((seqs, group)),
-            dma((n_pos,)),
-            dma((n_pos,)),
-            dma((n_head,)),
-            dma((n_head,)),
+            dma((n_pos * n_head,)),
+            dma((n_pos * n_head,)),
             dma((6,)),
             dma((2,)),
+            pltpu.SemaphoreType.REGULAR((2,)),
         ],
         compiler_params=pltpu.CompilerParams(
             collective_id=0, has_side_effects=True, vmem_limit_bytes=60 * 1024 * 1024

time: 58.6 us -> 57.8 us (0.986)
  Pallas kernels: 54.2 us -> 53.5 us
    pallas_call x1, Pallas kernels: 54.2 us -> 53.5 us  [on_device(): pl.pallas_call(functools.partial(kernel, n_pos, n_head, group, seqs), out...]
where the time goes in v1:
time: 57.8 us; the launch traced here: 57.6 us
  Pallas kernels  53.5 us (93%)
  between operations  2.4 us (4%)
  local copies, waits for them, and re-layouts  1.78 us (3%)
    pallas_call x1, Pallas kernels, on_device(): pl.pallas_call(functools.partial(kernel, n_pos, n_head, group, seqs), out...  53.5 us
    unnamed x1, local copies, waits for them, and re-layouts  1.78 us

profile of v1, /device:TPU:0, one launch (start us, length us, event | category | flops | bytes accessed | tf_op | source)
XLA Modules:
  0.0 57.6 jit_solution(11570824575070318881)
XLA Ops:
  0.6 53.5 %shard_map.140 = (bf16[8,64,262]{2,1,0:T(8,128)(2,1)}, f32[1,1]{1,0:T(1,128)}) custom-call(bf16[8,64,768]{2,1,0:T(8,128)(2,1)} %queries.1, bf16[8,32,1280]{2,1,0:T(8,128)(2,1)} %latents.1, bf16[768,768]{1,0:T(8,128)(2,1)} %w_query_hbm.1, f32[1280]{0:T(1024)} %kv_gain.1, bf16[1280,1536]{1,0:T(8,128)(2,1)} %w_kv_hbm.1, bf16[768,768]{1,0:T(8,128)(2,1)} %w_out_hbm.1, ...), custom_call_target="tpu_custom_call" | custom-call | tf_op jit(solution)/shard_map/pallas_call | solution.py:431
  54.1 1.8 %copy.17 = bf16[8,64,262]{2,1,0:T(8,128)(2,1)} copy(bf16[8,64,262]{2,1,0:T(8,128)(2,1)} %get-tuple-element.8) | data formatting | bytes 536576

commit v2 on v1

--- a/solution.py
+++ b/solution.py
@@ -1,4 +1,5 @@
 import functools
+import math
 
 import jax
 import jax.numpy as jnp
@@ -8,15 +9,15 @@
 from jax.sharding import PartitionSpec as P
 
 HEADS = 8
-LAT_SPLIT = 1
-ROW_SPLIT = 1
+LAT_SPLIT = 2
+LANES = 128
 epsilon = 1e-05
 MESH = pl.DeviceIdType.MESH
 
 
-def layer_norm(field, gain):
-    centre = field - jnp.mean(field, axis=-1, keepdims=True)
-    spread = jnp.mean(centre * centre, axis=-1, keepdims=True)
+def layer_norm(field, gain, axis):
+    centre = field - jnp.mean(field, axis=axis, keepdims=True)
+    spread = jnp.mean(centre * centre, axis=axis, keepdims=True)
     return centre * lax.rsqrt(spread + epsilon) * gain
 
 
@@ -24,10 +25,15 @@
     return jnp.dot(left, right, preferred_element_type=jnp.float32)
 
 
-def dot_last(left, right):
-    return lax.dot_general(
-        left, right, (((1,), (1,)), ((), ())), preferred_element_type=jnp.float32
-    )
+def dot_parts(left, right, cut):
+    return jnp.concatenate([dot(left[:cut], right), dot(left[cut:], right)], axis=0)
+
+
+def head_span(h, head_dim):
+    low, high = h * head_dim, (h + 1) * head_dim
+    begin = low // LANES * LANES
+    end = -(-high // LANES) * LANES
+    return low, high, begin, end
 
 
 def kernel(
@@ -62,13 +68,31 @@
     w_up,
     w_down,
     w_vocab,
-    kv_buf,
+    w_query_t,
+    w_out_t,
+    w_up_t,
+    w_down_t,
+    gain_col,
+    bias_row,
+    bias_col,
+    x_t,
+    q_pad,
+    norm_buf,
+    k_buf,
+    v_t,
+    score_buf,
+    top_buf,
+    total_buf,
+    power_buf,
+    att_t,
+    turn_buf,
     logit_buf,
     acc,
     part_src,
     part_all,
     lat_send,
     lat_recv,
+    q_own,
     q_send,
     q_recv,
     t_send,
@@ -156,7 +180,7 @@
         copy.start()
         local.append(copy)
 
-    start_local(queries.at[pl.ds(mine * seqs, seqs)], q_buf.at[0], q_recv.at[0])
+    start_local(queries.at[pl.ds(mine * seqs, seqs)], q_buf.at[0], q_own)
     start_local(targets, t_buf.at[0], t_recv.at[0])
     start_local(mask, m_buf.at[0], m_recv.at[0])
     def lat_copy(k, i):
@@ -185,9 +209,11 @@
             device_id_type=MESH,
         )
 
-    def q_copy(k):
+    def q_copy(k, i):
         peer = lax.rem(mine + k, group)
-        return group_copy(k, q_stage.at[pl.ds(peer * seqs, seqs)], q_buf.at[k], q_send, q_recv)
+        return group_copy(
+            k, q_stage.at[peer * seqs + i], q_buf.at[k, i], q_send.at[i], q_recv.at[i]
+        )
 
     def t_copy(k):
         return group_copy(k, targets, t_buf.at[k], t_send, t_recv)
@@ -249,118 +275,147 @@
         start_local(src, dst, w_sem.at[index])
 
     for k in range(1, group):
-        q_copy(k).start()
         t_copy(k).start()
         m_copy(k).start()
-    for k in cross + inner:
-        lat_copy(k, 1).start()
-
-    for copy in local:
-        copy.wait()
-    for k in range(1, group):
-        q_copy(k).wait_recv()
-        t_copy(k).wait_recv()
-        m_copy(k).wait_recv()
+    for i in range(seqs):
+        if i > 0:
+            for k in cross:
+
+                @pl.when(jnp.logical_not(near(pos_peer(k))))
+                def third(k=k, i=i):
+                    lat_copy(k, i).start()
+
+        for k in range(1, group):
+            q_copy(k, i).start()
+        if i > 0:
+            for k in cross:
+
+                @pl.when(near(pos_peer(k)))
+                def fourth(k=k, i=i):
+                    lat_copy(k, i).start()
+
+            for k in inner:
+                lat_copy(k, i).start()
 
     rows_dev = q_buf.shape[2]
     width = q_buf.shape[3]
     rows_all = group * rows_dev
     lat_dev = lat_buf.shape[2]
-    lat_split, row_split = LAT_SPLIT, ROW_SPLIT
     lat_width = lat_buf.shape[3]
     head_dim = width // HEADS
-    scale_factor = float(head_dim) ** (-0.5)
+    power_scale = float(head_dim) ** (-0.5) * math.log2(math.e)
     vocab = w_vocab.shape[0]
-    lanes = 128
+
+    for copy in local:
+        copy.wait()
+    for raw, turned in (
+        (w_query, w_query_t),
+        (w_out, w_out_t),
+        (w_up, w_up_t),
+        (w_down, w_down_t),
+    ):
+        turned[...] = raw[...].T
+    gain_col[...] = jnp.broadcast_to(mlp_gain[...].reshape(1, width), (LANES, width)).T
+    turn_buf[...] = jnp.zeros_like(turn_buf)
+    bias_row[...] = jnp.zeros_like(bias_row)
+    bias_row[:, :vocab] = vocab_bias[...].reshape(1, vocab)
+    bias_col[...] = jnp.broadcast_to(bias_row[...], (LANES, bias_row.shape[1])).T
+
+    def wide(column):
+        return jnp.concatenate([column] * (rows_all // LANES), axis=1)
+
+    for k in range(1, group):
+        t_copy(k).wait_recv()
+        m_copy(k).wait_recv()
+
+    def prepare(i):
+        for k in range(1, group):
+            q_copy(k, i).wait_recv()
+        turned = q_buf[:, i].reshape(rows_all, width).T
+        x_t[i] = turned.astype(jnp.float32)
+        query_t = dot(w_query_t[...], turned).astype(jnp.bfloat16)
+        for h in range(HEADS):
+            low, high, begin, end = head_span(h, head_dim)
+            if low > begin:
+                q_pad[i, h, : low - begin] = jnp.zeros((low - begin, rows_all), jnp.bfloat16)
+            q_pad[i, h, low - begin : high - begin] = query_t[low:high]
+            if end > high:
+                q_pad[i, h, high - begin : end - begin] = jnp.zeros(
+                    (end - high, rows_all), jnp.bfloat16
+                )
+
     acc[...] = jnp.zeros_like(acc)
 
-    columns = []
-    for k in range(group):
-        code = (t_buf[k] + vocab * m_buf[k]).astype(jnp.float32)
-        pad = -rows_dev % lanes
-        if pad:
-            code = jnp.concatenate(
-                [code, jnp.zeros((code.shape[0], pad), jnp.float32)], axis=1
-            )
-        columns.append(code.T[:rows_dev])
-    code_cols = jnp.concatenate(columns, axis=0)
+    slots = n_pos // LAT_SPLIT
+    lat_rows = slots * lat_dev
+    some = max(1, min(slots, 64 // lat_dev))
+    chunk = 256
 
     def one_sequence(i, carry):
-        seq_queries = q_buf[:, i].reshape(rows_all, width)
-        query_all = dot(seq_queries, w_query[...]).astype(jnp.bfloat16)
-
-        chunk = 256
-        step = n_pos // lat_split
-        lat_rows = step * lat_dev
-        for part in reversed(range(lat_split)):
-            for k in reversed(range(part * step, (part + 1) * step)):
-                if k == 0:
-                    lat_local(i).wait()
+        prepare(i)
+        for part in reversed(range(LAT_SPLIT)):
+            base_row = part * lat_rows
+            for start in range(part * slots, (part + 1) * slots, some):
+                for k in range(start, start + some):
+                    if k == 0:
+                        lat_local(i).wait()
+                    else:
+                        lat_copy(k, i).wait_recv()
+                field = lat_buf[i, start : start + some].astype(jnp.float32)
+                field = field.reshape(some * lat_dev, lat_width)
+                norm_buf[start * lat_dev : (start + some) * lat_dev] = layer_norm(
+                    field, kv_gain[...].reshape(1, lat_width), 1
+                ).astype(jnp.bfloat16)
+            normed_lat = norm_buf[base_row : base_row + lat_rows]
+            for start in range(0, 2 * width, chunk):
+                block_kv = dot(normed_lat, w_kv[:, start : start + chunk]).astype(jnp.bfloat16)
+                if start < width:
+                    k_buf[base_row : base_row + lat_rows, start : start + chunk] = block_kv
                 else:
-                    lat_copy(k, i).wait_recv()
-            field = lat_buf[i, part * step : (part + 1) * step].astype(jnp.float32)
-            field = field.reshape(lat_rows, lat_width)
-            normed_lat = layer_norm(field, kv_gain[...].reshape(1, lat_width)).astype(jnp.bfloat16)
-            for start in range(0, 2 * width, chunk):
-                kv_buf[part * lat_rows : (part + 1) * lat_rows, start : start + chunk] = dot(
-                    normed_lat, w_kv[:, start : start + chunk]
-                ).astype(jnp.bfloat16)
-
-        for part in reversed(range(row_split)):
-            decode(i, part, query_all)
-        return carry
-
-    def decode(i, part, query_all):
-        members = group // row_split
-        begin_slot = part * members
-        rows = members * rows_dev
-        begin_row = begin_slot * rows_dev
-        query_proj = query_all[begin_row : begin_row + rows]
-        seq_queries = q_buf[begin_slot : begin_slot + members, i].reshape(rows, width)
-        code_all = code_cols[begin_row : begin_row + rows]
-
-        tiles = [None] * (width // lanes)
+                    v_t[start - width : start - width + chunk, base_row : base_row + lat_rows] = (
+                        block_kv.T
+                    )
+
+        for h in range(HEADS):
+            low, high, begin, end = head_span(h, head_dim)
+            scores = dot(k_buf[:, begin:end], q_pad[i, h, : end - begin])
+            score_buf[h] = scores
+            top_buf[h : h + 1] = jnp.max(scores, axis=0, keepdims=True)
+        for h in range(HEADS):
+            power = jnp.exp2((score_buf[h] - top_buf[h : h + 1]) * power_scale)
+            total_buf[h : h + 1] = jnp.sum(power, axis=0, keepdims=True)
+            power_buf[h] = power.astype(jnp.bfloat16)
         for h in range(HEADS):
             low, high = h * head_dim, (h + 1) * head_dim
-            first_tile, last_tile = low // lanes, (high - 1) // lanes
-            begin, end = first_tile * lanes, (last_tile + 1) * lanes
-            lane = lax.broadcasted_iota(jnp.int32, (1, end - begin), 1) + begin
-            inside = jnp.logical_and(lane >= low, lane < high).astype(jnp.bfloat16)
-            keys = kv_buf[:, begin:end] * inside
-            values = kv_buf[:, width + begin : width + end] * inside
-            scores = (
-                dot_last(query_proj[:, begin:end], keys) * scale_factor
-            )
-            power = jnp.exp(scores - jnp.max(scores, axis=-1, keepdims=True))
-            weights = (power / jnp.sum(power, axis=-1, keepdims=True)).astype(jnp.bfloat16)
-            part = dot(weights, values)
-            for t in range(first_tile, last_tile + 1):
-                piece = part[:, t * lanes - begin : (t + 1) * lanes - begin]
-                tiles[t] = piece if tiles[t] is None else tiles[t] + piece
-        attended = jnp.concatenate([tile.astype(jnp.bfloat16) for tile in tiles], axis=1)
-
-        first = seq_queries.astype(jnp.float32) + dot(attended, w_out[...])
-        normed = layer_norm(first, mlp_gain[...].reshape(1, width)).astype(jnp.bfloat16)
-        hidden = jax.nn.gelu(dot(normed, w_up[...])).astype(jnp.bfloat16)
-        output = (first + dot(hidden, w_down[...])).astype(jnp.bfloat16)
-        full_logits = dot_last(output, w_vocab[...]) + vocab_bias[...].reshape(1, vocab)
-        logit_buf[i, begin_slot : begin_slot + members] = full_logits.astype(jnp.bfloat16).reshape(
-            members, rows_dev, vocab
-        )
-
-        code_lane = lax.broadcasted_iota(jnp.int32, code_all.shape, 1)
-        code = jnp.sum(
-            jnp.where(code_lane == mine * seqs + i, code_all, 0.0), axis=1, keepdims=True
-        )
-        weight_mask = (code >= float(vocab)).astype(jnp.float32)
-        target = (code - float(vocab) * weight_mask).astype(jnp.int32)
-        ids = lax.broadcasted_iota(jnp.int32, full_logits.shape, 1)
-        picked = jnp.sum(jnp.where(ids == target, full_logits, 0.0), axis=1, keepdims=True)
-        top = jnp.max(full_logits, axis=1, keepdims=True)
-        spread = jnp.log(jnp.sum(jnp.exp(full_logits - top), axis=1, keepdims=True))
-        cross = top + spread - picked
-
-        for k in range(begin_slot, begin_slot + members):
+            mixed = dot(v_t[low:high], power_buf[h])
+            att_t[low:high] = (mixed * (1.0 / total_buf[h : h + 1])).astype(jnp.bfloat16)
+
+        half = width // 2
+        first = x_t[i] + dot_parts(w_out_t, att_t[...], half)
+        normed = layer_norm(first, wide(gain_col[...]), 0).astype(jnp.bfloat16)
+        hidden = jax.nn.gelu(dot_parts(w_up_t, normed, half)).astype(jnp.bfloat16)
+        output = (first + dot_parts(w_down_t, hidden, half)).astype(jnp.bfloat16)
+        full_logits = dot_parts(w_vocab, output, LANES) + wide(bias_col[:vocab])
+        turn_buf[:vocab] = full_logits
+        logit_buf[i] = (
+            turn_buf[...].T[:, :vocab].astype(jnp.bfloat16).reshape(group, rows_dev, vocab)
+        )
+
+        line = mine * seqs + i
+        target = jnp.concatenate([t_buf[k, pl.ds(line, 1)] for k in range(group)], axis=1)
+        weight = jnp.concatenate([m_buf[k, pl.ds(line, 1)] for k in range(group)], axis=1)
+        weight = weight.astype(jnp.float32)
+        ids = lax.broadcasted_iota(jnp.int32, full_logits.shape, 0)
+        picked = jnp.sum(jnp.where(ids == target, full_logits, 0.0), axis=0, keepdims=True)
+        top = jnp.max(full_logits, axis=0, keepdims=True)
+        spread = jnp.log(jnp.sum(jnp.exp(full_logits - top), axis=0, keepdims=True))
+        cross_loss = (top + spread - picked) * weight
+        for start in range(0, rows_all, LANES):
+            acc[:, :LANES] += cross_loss[:, start : start + LANES]
+            acc[:, LANES:] += weight[:, start : start + LANES]
+
+        for k in range(group):
+
             @pl.when(i < seqs - 1)
             def send(k=k):
                 if k == 0:
@@ -368,10 +423,7 @@
                 else:
                     out_copy(k, i).start()
 
-        loss_sum = jnp.sum(cross * weight_mask, axis=0, keepdims=True)
-        mask_sum = jnp.sum(weight_mask, axis=0, keepdims=True)
-        place = lax.broadcasted_iota(jnp.int32, acc.shape, 1)
-        acc[...] += jnp.where(place == 0, loss_sum, jnp.where(place == 1, mask_sum, 0.0))
+        return carry
 
     lax.fori_loop(0, seqs, one_sequence, 0)
 
@@ -400,12 +452,15 @@
     for k in range(1, n_all):
         p_copy(k).wait_recv()
     whole = jnp.sum(part_all[...], axis=0)
-    loss_out[...] = whole[:, 0:1] / whole[:, 1:2]
+    loss_out[...] = jnp.sum(whole[:, :LANES], axis=1, keepdims=True) / jnp.sum(
+        whole[:, LANES:], axis=1, keepdims=True
+    )
 
     for k in range(1, n_all):
         p_copy(k).wait_send()
     for k in range(1, group):
-        q_copy(k).wait_send()
+        for i in range(seqs):
+            q_copy(k, i).wait_send()
         t_copy(k).wait_send()
         m_copy(k).wait_send()
     for i in range(seqs):
@@ -424,6 +479,9 @@
     group = max(1, min(n_pos, batch_dev) // 2)
     seqs = batch_dev // group
     assert n_pos % group == 0 and batch_dev % group == 0
+    rows_all = group * pos_dev
+    assert rows_all % LANES == 0 and n_pos % LAT_SPLIT == 0
+    vocab_pad = -(-vocab // LANES) * LANES
     hbm = pl.BlockSpec(memory_space=pltpu.HBM)
     vmem = pl.BlockSpec(memory_space=pltpu.VMEM)
     dma = pltpu.SemaphoreType.DMA
@@ -449,15 +507,33 @@
             pltpu.VMEM(w_up.shape, bf16),
             pltpu.VMEM(w_down.shape, bf16),
             pltpu.VMEM(w_vocab.shape[::-1], bf16),
-            pltpu.VMEM((n_pos * lat_dev, 2 * width), bf16),
+            pltpu.VMEM(w_query.shape[::-1], bf16),
+            pltpu.VMEM(w_out.shape[::-1], bf16),
+            pltpu.VMEM(w_up.shape[::-1], bf16),
+            pltpu.VMEM(w_down.shape[::-1], bf16),
+            pltpu.VMEM((width, LANES), f32),
+            pltpu.VMEM((1, vocab_pad), f32),
+            pltpu.VMEM((vocab_pad, LANES), f32),
+            pltpu.VMEM((seqs, width, rows_all), f32),
+            pltpu.VMEM((seqs, HEADS, 2 * LANES, rows_all), bf16),
+            pltpu.VMEM((n_pos * lat_dev, lat_width), bf16),
+            pltpu.VMEM((n_pos * lat_dev, width), bf16),
+            pltpu.VMEM((width, n_pos * lat_dev), bf16),
+            pltpu.VMEM((HEADS, n_pos * lat_dev, rows_all), f32),
+            pltpu.VMEM((HEADS, rows_all), f32),
+            pltpu.VMEM((HEADS, rows_all), f32),
+            pltpu.VMEM((HEADS, n_pos * lat_dev, rows_all), bf16),
+            pltpu.VMEM((width, rows_all), bf16),
+            pltpu.VMEM((vocab_pad, rows_all), f32),
             pltpu.VMEM((seqs, group, pos_dev, vocab), bf16),
-            pltpu.VMEM((1, 128), f32),
-            pltpu.VMEM((1, 128), f32),
-            pltpu.VMEM((n_pos * n_head, 1, 128), f32),
+            pltpu.VMEM((1, 2 * LANES), f32),
+            pltpu.VMEM((1, 2 * LANES), f32),
+            pltpu.VMEM((n_pos * n_head, 1, 2 * LANES), f32),
             dma((seqs, n_pos)),
             dma((seqs, n_pos)),
-            dma((group,)),
-            dma((group,)),
+            pltpu.SemaphoreType.DMA,
+            dma((seqs, group)),
+            dma((seqs, group)),
             dma((group,)),
             dma((group,)),
             dma((group,)),

time: 57.8 us -> 53.5 us (0.926)
  Pallas kernels: 53.5 us -> 49.1 us
    pallas_call x1, Pallas kernels: 53.5 us -> 49.1 us  [on_device(): pl.pallas_call(functools.partial(kernel, n_pos, n_head, group, seqs), out...]
where the time goes in v2:
time: 53.5 us; the launch traced here: 53.3 us
  Pallas kernels  49.1 us (92%)
  between operations  2.4 us (4%)
  local copies, waits for them, and re-layouts  1.78 us (3%)
    pallas_call x1, Pallas kernels, on_device(): pl.pallas_call(functools.partial(kernel, n_pos, n_head, group, seqs), out...  49.1 us
    unnamed x1, local copies, waits for them, and re-layouts  1.78 us

profile of v2, /device:TPU:0, one launch (start us, length us, event | category | flops | bytes accessed | tf_op | source)
XLA Modules:
  0.0 53.3 jit_solution(561436542398137249)
XLA Ops:
  0.6 49.1 %shard_map.140 = (bf16[8,64,262]{2,1,0:T(8,128)(2,1)}, f32[1,1]{1,0:T(1,128)}) custom-call(bf16[8,64,768]{2,1,0:T(8,128)(2,1)} %queries.1, bf16[8,32,1280]{2,1,0:T(8,128)(2,1)} %latents.1, bf16[768,768]{1,0:T(8,128)(2,1)} %w_query_hbm.1, f32[1280]{0:T(1024)} %kv_gain.1, bf16[1280,1536]{1,0:T(8,128)(2,1)} %w_kv_hbm.1, bf16[768,768]{1,0:T(8,128)(2,1)} %w_out_hbm.1, ...), custom_call_target="tpu_custom_call" | custom-call | tf_op jit(solution)/shard_map/pallas_call | solution.py:489
  49.7 1.8 %copy.17 = bf16[8,64,262]{2,1,0:T(8,128)(2,1)} copy(bf16[8,64,262]{2,1,0:T(8,128)(2,1)} %get-tuple-element.8) | data formatting | bytes 536576

commit v3 on v2

--- a/solution.py
+++ b/solution.py
@@ -351,8 +351,21 @@
     some = max(1, min(slots, 64 // lat_dev))
     chunk = 256
 
+    def hand_over(i):
+        logit_buf[i] = (
+            turn_buf[i].T[:, :vocab].astype(jnp.bfloat16).reshape(group, rows_dev, vocab)
+        )
+        for k in range(1, group):
+            out_copy(k, i).start()
+        out_local(i).start()
+
     def one_sequence(i, carry):
         prepare(i)
+
+        @pl.when(i > 0)
+        def earlier():
+            hand_over(i - 1)
+
         for part in reversed(range(LAT_SPLIT)):
             base_row = part * lat_rows
             for start in range(part * slots, (part + 1) * slots, some):
@@ -396,11 +409,7 @@
         hidden = jax.nn.gelu(dot_parts(w_up_t, normed, half)).astype(jnp.bfloat16)
         output = (first + dot_parts(w_down_t, hidden, half)).astype(jnp.bfloat16)
         full_logits = dot_parts(w_vocab, output, LANES) + wide(bias_col[:vocab])
-        turn_buf[:vocab] = full_logits
-        logit_buf[i] = (
-            turn_buf[...].T[:, :vocab].astype(jnp.bfloat16).reshape(group, rows_dev, vocab)
-        )
-
+        turn_buf[i, :vocab] = full_logits
         line = mine * seqs + i
         target = jnp.concatenate([t_buf[k, pl.ds(line, 1)] for k in range(group)], axis=1)
         weight = jnp.concatenate([m_buf[k, pl.ds(line, 1)] for k in range(group)], axis=1)
@@ -414,15 +423,6 @@
             acc[:, :LANES] += cross_loss[:, start : start + LANES]
             acc[:, LANES:] += weight[:, start : start + LANES]
 
-        for k in range(group):
-
-            @pl.when(i < seqs - 1)
-            def send(k=k):
-                if k == 0:
-                    out_local(i).start()
-                else:
-                    out_copy(k, i).start()
-
         return carry
 
     lax.fori_loop(0, seqs, one_sequence, 0)
@@ -430,8 +430,20 @@
     n_all = n_pos * n_head
     rank = me * n_head + my_head
 
+    swaps = [k // 2 if k % 2 == 0 else n_all - 1 - k // 2 for k in range(n_all)]
+
+    def p_peer(k):
+        return lax.rem(2 * n_all - 1 - rank + k, n_all)
+
+    def p_each(act):
+        for k in swaps:
+
+            @pl.when(p_peer(k) != rank)
+            def other(k=k):
+                act(p_copy(k))
+
     def p_copy(k):
-        peer = lax.rem(rank + k, n_all)
+        peer = p_peer(k)
         return pltpu.make_async_remote_copy(
             src_ref=part_src,
             dst_ref=part_all.at[rank],
@@ -444,20 +456,15 @@
     part = acc[...]
     part_src[...] = part
     part_all[rank] = part
-    for k in range(1, n_all):
-        p_copy(k).start()
-    for k in range(1, group):
-        out_copy(k, seqs - 1).start()
-    out_local(seqs - 1).start()
-    for k in range(1, n_all):
-        p_copy(k).wait_recv()
+    p_each(lambda copy: copy.start())
+    hand_over(seqs - 1)
+    p_each(lambda copy: copy.wait_recv())
     whole = jnp.sum(part_all[...], axis=0)
     loss_out[...] = jnp.sum(whole[:, :LANES], axis=1, keepdims=True) / jnp.sum(
         whole[:, LANES:], axis=1, keepdims=True
     )
 
-    for k in range(1, n_all):
-        p_copy(k).wait_send()
+    p_each(lambda copy: copy.wait_send())
     for k in range(1, group):
         for i in range(seqs):
             q_copy(k, i).wait_send()
@@ -489,11 +496,11 @@
     logits, loss = pl.pallas_call(
         functools.partial(kernel, n_pos, n_head, group, seqs),
         out_shape=(
-            jax.ShapeDtypeStruct((batch_dev, pos_dev, vocab), bf16),
-            jax.ShapeDtypeStruct((1, 1), f32),
+            pltpu.VMEM((batch_dev, pos_dev, vocab), bf16),
+            pltpu.VMEM((1, 1), f32),
         ),
         in_specs=[hbm, hbm, hbm, vmem, hbm, hbm, vmem, hbm, hbm, hbm, vmem, hbm, hbm],
-        out_specs=(pl.BlockSpec(memory_space=pl.ANY), vmem),
+        out_specs=(vmem, vmem),
         scratch_shapes=[
             pltpu.VMEM(latents.shape, bf16),
             pltpu.VMEM(queries.shape, bf16),
@@ -524,7 +531,7 @@
             pltpu.VMEM((HEADS, rows_all), f32),
             pltpu.VMEM((HEADS, n_pos * lat_dev, rows_all), bf16),
             pltpu.VMEM((width, rows_all), bf16),
-            pltpu.VMEM((vocab_pad, rows_all), f32),
+            pltpu.VMEM((seqs, vocab_pad, rows_all), f32),
             pltpu.VMEM((seqs, group, pos_dev, vocab), bf16),
             pltpu.VMEM((1, 2 * LANES), f32),
             pltpu.VMEM((1, 2 * LANES), f32),

time: 53.5 us -> 51.3 us (0.959)
  local copies, waits for them, and re-layouts: 1.78 us -> 0.75 us
  between operations: 2.4 us -> 1.81 us
    unnamed x1, local copies, waits for them, and re-layouts: 1.78 us -> 0.75 us
where the time goes in v3:
time: 51.3 us; the launch traced here: 51.1 us
  Pallas kernels  48.6 us (95%)
  between operations  1.81 us (4%)
  local copies, waits for them, and re-layouts  0.75 us (1%)
    pallas_call x1, Pallas kernels, on_device(): pl.pallas_call(functools.partial(kernel, n_pos, n_head, group, seqs), out...  48.6 us

profile of v3, /device:TPU:0, one launch (start us, length us, event | category | flops | bytes accessed | tf_op | source)
XLA Modules:
  0.0 51.1 jit_solution(9323680958586321260)
XLA Ops:
  0.6 48.6 %shard_map.140 = (bf16[8,64,262]{2,1,0:T(8,128)(2,1)S(1)}, f32[1,1]{1,0:T(1,128)S(1)}) custom-call(bf16[8,64,768]{2,1,0:T(8,128)(2,1)} %queries.1, bf16[8,32,1280]{2,1,0:T(8,128)(2,1)} %latents.1, bf16[768,768]{1,0:T(8,128)(2,1)} %w_query_hbm.1, f32[1280]{0:T(1024)} %kv_gain.1, bf16[1280,1536]{1,0:T(8,128)(2,1)} %w_kv_hbm.1, bf16[768,768]{1,0:T(8,128)(2,1)} %w_out_hbm.1, ...), custom_call_target="tpu_custom_call" | custom-call | tf_op jit(solution)/shard_map/pallas_call | solution.py:496
  49.2 0.7 %copy.17 = bf16[8,64,262]{2,1,0:T(8,128)(2,1)} copy(bf16[8,64,262]{2,1,0:T(8,128)(2,1)S(1)} %get-tuple-element.6) | data formatting | bytes 536576

commit v4 on v3

--- a/solution.py
+++ b/solution.py
@@ -460,9 +460,10 @@
     hand_over(seqs - 1)
     p_each(lambda copy: copy.wait_recv())
     whole = jnp.sum(part_all[...], axis=0)
-    loss_out[...] = jnp.sum(whole[:, :LANES], axis=1, keepdims=True) / jnp.sum(
+    mean = jnp.sum(whole[:, :LANES], axis=1, keepdims=True) / jnp.sum(
         whole[:, LANES:], axis=1, keepdims=True
     )
+    loss_out[...] = jnp.broadcast_to(mean, loss_out.shape)
 
     p_each(lambda copy: copy.wait_send())
     for k in range(1, group):
@@ -476,6 +477,13 @@
         out_local(i).wait()
         for k in range(1, group):
             out_copy(k, i).wait()
+
+
+def deliver(logits, loss, logits_out, loss_out, sems):
+    copy = pltpu.make_async_copy(logits, logits_out, sems.at[0])
+    copy.start()
+    loss_out[...] = loss[0:1, 0:1]
+    copy.wait()
 
 
 def on_device(n_pos, n_head, *args):
@@ -497,7 +505,7 @@
         functools.partial(kernel, n_pos, n_head, group, seqs),
         out_shape=(
             pltpu.VMEM((batch_dev, pos_dev, vocab), bf16),
-            pltpu.VMEM((1, 1), f32),
+            pltpu.VMEM((8, LANES), f32),
         ),
         in_specs=[hbm, hbm, hbm, vmem, hbm, hbm, vmem, hbm, hbm, hbm, vmem, hbm, hbm],
         out_specs=(vmem, vmem),
@@ -571,6 +579,17 @@
         targets,
         mask,
     )
+    logits, loss = pl.pallas_call(
+        deliver,
+        out_shape=(
+            jax.ShapeDtypeStruct((batch_dev, pos_dev, vocab), bf16),
+            jax.ShapeDtypeStruct((1, 1), f32),
+        ),
+        in_specs=[pl.BlockSpec(memory_space=pl.ANY), vmem],
+        out_specs=(hbm, vmem),
+        scratch_shapes=[pltpu.SemaphoreType.DMA((2,))],
+        compiler_params=pltpu.CompilerParams(vmem_limit_bytes=1024 * 1024),
+    )(logits, loss)
     return (logits, loss.reshape(()))
 
 

time: 51.3 us -> 50.7 us (0.988)
  Pallas kernels: 48.6 us -> 49.8 us
  between operations: 1.81 us -> 0.64 us
  local copies, waits for them, and re-layouts: 0.75 us -> 0 us
    pallas_call x0 -> x1, Pallas kernels: none -> 1.27 us  [on_device(): pl.pallas_call(deliver, out_shape=(jax.ShapeDtypeStruct((batch_dev, pos_d...]
    unnamed x1 -> x0, local copies, waits for them, and re-layouts: 0.75 us -> none
where the time goes in v4:
time: 50.7 us; the launch traced here: 50.5 us
  Pallas kernels  49.8 us (98%)
  between operations  0.64 us (1%)
    pallas_call x1, Pallas kernels, on_device(): pl.pallas_call(functools.partial(kernel, n_pos, n_head, group, seqs), out...  48.6 us
    pallas_call x1, Pallas kernels, on_device(): pl.pallas_call(deliver, out_shape=(jax.ShapeDtypeStruct((batch_dev, pos_d...  1.27 us

profile of v4, /device:TPU:0, one launch (start us, length us, event | category | flops | bytes accessed | tf_op | source)
XLA Modules:
  0.0 50.5 jit_solution(12532775272425648023)
XLA Ops:
  0.6 48.6 %shard_map.140 = (bf16[8,64,262]{2,1,0:T(8,128)(2,1)S(1)}, f32[8,128]{1,0:T(8,128)S(1)}) custom-call(bf16[8,64,768]{2,1,0:T(8,128)(2,1)} %queries.1, bf16[8,32,1280]{2,1,0:T(8,128)(2,1)} %latents.1, bf16[768,768]{1,0:T(8,128)(2,1)} %w_query_hbm.1, f32[1280]{0:T(1024)} %kv_gain.1, bf16[1280,1536]{1,0:T(8,128)(2,1)} %w_kv_hbm.1, bf16[768,768]{1,0:T(8,128)(2,1)} %w_out_hbm.1, ...), custom_call_target="tpu_custom_call" | custom-call | tf_op jit(solution)/shard_map/pallas_call | solution.py:504
  49.2 1.3 %shard_map.141 = (bf16[8,64,262]{2,1,0:T(8,128)(2,1)}, f32[1,1]{1,0:T(1,128)}) custom-call(bf16[8,64,262]{2,1,0:T(8,128)(2,1)S(1)} %get-tuple-element.6.logits, f32[8,128]{1,0:T(8,128)S(1)} %get-tuple-element.7.loss), custom_call_target="tpu_custom_call" | custom-call | tf_op jit(solution)/shard_map/pallas_call | solution.py:582
